TPU v7x, 32 devices: a whole 2x2x4 slice. The times are simulated.
32 devices in a mesh: feed: 8 (over y, x, core), band: 4 (over z).
Axes of the slice: x: 2, y: 2, z: 4, core: 2. Of those that a mesh axis runs over, the one named last changes fastest.
Arguments:
- voltages: int32 [4, 8, 1024, 512], P('band', None, 'feed'), may hold values from -2147483648 to 2147483646
- complex_gains: float32 [2, 4, 8, 1024], P(None, 'band', None, 'feed'), may hold values from -4 to 4
- channel_map: int32 [4, 8], P('band'), may hold values from 0 to 7, each once within a row
Outputs:
- visibility: float32 [2, 4, 8, 1024, 1024], P(None, 'band', 'feed')
Inputs may be any that keep to these rules, and one draw needn't show every extreme that they name: `channel_map`: each sub-band's row is a permutation of 0 to 7.
All inputs are finite; a program needn't handle non-finite values.
Results may differ from a plain program's by a relative error of at most 0.0003.
Values sent between devices are 32-bit elements; how exact they have to be, the bound alone decides.
A program may use at most 128 MiB of HBM per device.

v0:
```python
import functools

import jax
import jax.numpy as jnp
from jax import lax
from jax.experimental import pallas as pl
from jax.experimental.pallas import tpu as pltpu
from jax.sharding import PartitionSpec as P

MESH = pl.DeviceIdType.MESH
PLANE = jnp.bfloat16
BLOCK = 128
LANES = 128


def flip(index, mask, size):
    total, bit = 0, 1
    while bit < size:
        digit = lax.rem(index // bit, 2)
        total = total + ((1 - digit) if mask & bit else digit) * bit
        bit *= 2
    return total


def weigh(gram, col, row):
    gram_re = gram[:BLOCK, :BLOCK] + gram[BLOCK:, BLOCK:]
    gram_im = gram[BLOCK:, :BLOCK] - gram[:BLOCK, BLOCK:]
    col_re, col_im = col[:, 0:1], col[:, 1:2]
    row_re, row_im = row[0:1, :], row[1:2, :]
    weight_re = col_re * row_re + col_im * row_im
    weight_im = col_im * row_re - col_re * row_im
    return weight_re * gram_re - weight_im * gram_im, weight_re * gram_im + weight_im * gram_re


def product(left, right):
    return lax.dot_general(left, right, (((1,), (1,)), ((), ())), preferred_element_type=jnp.float32)


def send_order(n):
    return sorted(range(1, n), key=lambda m: (m & (m - 1) > 1 and bin(m >> 1).count("1") > 1, m & 1, m))


def gather_kernel(n, scale, map_hbm, volt_hbm, gain_hbm, vis_ref, planes, acc, gcols, grows,
                  map_ref, gain_ref, volt, stage, gstage, recv, grecv,
                  map_sem, gain_sem, load_sem, send_sem, recv_sem, gsend_sem, grecv_sem):
    me = lax.axis_index("feed")
    rows, words = volt.shape[1], volt.shape[2]
    per_group = BLOCK // rows
    groups = n // per_group
    chunks = words // LANES
    low = lax.rem(me, per_group)
    own_group = me // per_group
    last = groups - 1

    map_copy = pltpu.make_async_copy(map_hbm, map_ref, map_sem)
    gain_copy = pltpu.make_async_copy(gain_hbm, gain_ref, gain_sem)
    load = pltpu.make_async_copy(volt_hbm.at[0], volt, load_sem)
    map_copy.start()
    gain_copy.start()
    load.start()
    barrier = pltpu.get_barrier_semaphore()
    for mask in range(1, n):
        pl.semaphore_signal(barrier, inc=1, device_id={"feed": flip(me, mask, n)}, device_id_type=MESH)
    map_copy.wait()
    gain_copy.wait()
    for mask in range(n):
        channel = map_ref[0, flip(me, mask, n)]
        for part in range(2):
            gstage[mask, part:part + 1, :] = gain_ref[part, pl.ds(channel, 1), :]
    load.wait()
    order = send_order(n)
    first, rest = order[:2], order[2:]
    for mask in first:
        stage[mask] = volt[map_ref[0, flip(me, mask, n)]]
    pl.semaphore_wait(barrier, n - 1)

    copies = []

    def send(source, target, sent, landed, mask):
        copies.append(pltpu.make_async_remote_copy(
            src_ref=source, dst_ref=target, send_sem=sent, recv_sem=landed,
            device_id={"feed": flip(me, mask, n)}, device_id_type=MESH))
        copies[-1].start()

    def send_whole(masks):
        for mask in masks:
            place = (mask // per_group) * per_group + low
            if mask // per_group < last:
                send(stage.at[mask], recv.at[place], send_sem.at[mask, 0], recv_sem.at[place, 0], mask)

    for mask in order:
        place = (mask // per_group) * per_group + low
        send(gstage.at[mask], grecv.at[place], gsend_sem.at[mask], grecv_sem.at[place], mask)
    send_whole(first)
    for mask in rest:
        stage[mask] = volt[map_ref[0, flip(me, mask, n)]]
    send_whole(rest)
    for c in range(chunks):
        part = pl.ds(c * LANES, LANES)
        for mask in order:
            place = (mask // per_group) * per_group + low
            if mask // per_group == last:
                send(stage.at[mask, :, part], recv.at[place, :, part], send_sem.at[mask, c],
                     recv_sem.at[place, c], mask)
    recv[low] = volt[map_ref[0, me]]
    grecv[low] = gstage[0]

    def places(group):
        return [group * per_group + flip(low, t, per_group) for t in range(per_group) if group or t]

    def unpack(group, c):
        step = 32
        part_of = pl.ds(c * LANES, LANES)

        def piece(i, carry):
            start = pl.multiple_of(i * step, step)
            if rows >= step:
                packed = recv[group, pl.ds(start, step), part_of]
            else:
                first = group * per_group + i * (step // rows)
                packed = recv[pl.ds(first, step // rows), :, part_of].reshape(step, LANES)
            for k in range(4):
                for part in range(2):
                    field = jnp.right_shift(jnp.left_shift(packed, 28 - 8 * k - 4 * part), 28)
                    column = (4 * c + k) * LANES
                    planes[group, pl.ds(part * BLOCK + start, step), column:column + LANES] = (
                        field.astype(jnp.float32).astype(PLANE))
            return carry

        lax.fori_loop(0, BLOCK // step, piece, 0)

    for group in range(groups):
        for place in places(group):
            pltpu.make_async_copy(grecv.at[place], grecv.at[place], grecv_sem.at[place]).wait()
        gains = grecv[group * per_group]
        for t in range(1, per_group):
            gains = gains + grecv[group * per_group + t]
        grows[group] = gains
        gcols[group] = jnp.transpose(jnp.concatenate([gains * scale] + [jnp.zeros_like(gains)] * 3, axis=0))

    arrivals = []
    for mask in [0] + order:
        if mask // per_group not in arrivals and mask // per_group < last:
            arrivals.append(mask // per_group)
    for position, group in enumerate(arrivals):
        for place in places(group):
            pltpu.make_async_copy(recv.at[place], recv.at[place], recv_sem.at[place, 0]).wait()
        for c in range(chunks):
            unpack(group, c)
        top = pl.multiple_of(flip(own_group, group, groups) * BLOCK, BLOCK)
        for other in arrivals[:position + 1]:
            left = pl.multiple_of(flip(own_group, other, groups) * BLOCK, BLOCK)
            vis_re, vis_im = weigh(product(planes[group], planes[other]), gcols[group], grows[other])
            vis_ref[0, pl.ds(top, BLOCK), pl.ds(left, BLOCK)] = vis_re
            vis_ref[1, pl.ds(top, BLOCK), pl.ds(left, BLOCK)] = vis_im
            if other != group:
                vis_ref[0, pl.ds(left, BLOCK), pl.ds(top, BLOCK)] = jnp.transpose(vis_re)
                vis_ref[1, pl.ds(left, BLOCK), pl.ds(top, BLOCK)] = jnp.transpose(-vis_im)

    for c in range(chunks):
        for place in places(last):
            here = recv.at[place, :, pl.ds(c * LANES, LANES)]
            pltpu.make_async_copy(here, here, recv_sem.at[place, c]).wait()
        unpack(last, c)
        span = pl.ds(4 * c * LANES, 4 * LANES)
        if c < chunks - 1:
            for other in range(groups):
                term = product(planes[last, :, span], planes[other, :, span])
                acc[other] = term if c == 0 else acc[other] + term

    for copy in copies:
        copy.wait_send()


def write_kernel(vis_ref, planes, acc, gcols, grows, out_hbm, row_strip, column_strip, sems):
    groups = planes.shape[0]
    per_group = lax.axis_size("feed") // groups
    own_group = lax.axis_index("feed") // per_group
    last = groups - 1
    span = pl.ds(planes.shape[2] - 4 * LANES, 4 * LANES)

    def spot(group):
        return pl.ds(pl.multiple_of(flip(own_group, group, groups) * BLOCK, BLOCK), BLOCK)

    copies = []

    def write(source, rows, columns):
        copies.append(pltpu.make_async_copy(source, out_hbm.at[:, rows, columns], sems.at[len(copies)]))
        copies[-1].start()

    for group in range(last):
        size = groups // 2
        while size:
            prefix = groups - 2 * size
            start = flip(own_group, prefix, groups) // size * size
            columns = pl.ds(pl.multiple_of(start * BLOCK, BLOCK), size * BLOCK)
            write(vis_ref.at[:, spot(group), columns], spot(group), columns)
            size //= 2
    for other in range(groups):
        gram = acc[other] + product(planes[last, :, span], planes[other, :, span])
        vis_re, vis_im = weigh(gram, gcols[last], grows[other])
        row_strip[other, 0] = vis_re
        row_strip[other, 1] = vis_im
        write(row_strip.at[other], spot(last), spot(other))
        if other < last:
            column_strip[other, 0] = jnp.transpose(vis_re)
            column_strip[other, 1] = jnp.transpose(-vis_im)
            write(column_strip.at[other], spot(other), spot(last))
    for copy in copies:
        copy.wait()


def body(voltages, complex_gains, channel_map):
    n = lax.axis_size("feed")
    slots, rows, words = voltages.shape[1:]
    feeds = rows * n
    gains = complex_gains[:, 0]
    per_group = BLOCK // rows
    if per_group > 1:
        low = lax.rem(lax.axis_index("feed"), per_group)
        gains = lax.dynamic_update_slice(jnp.zeros((2, slots, BLOCK), gains.dtype), gains, (0, 0, low * rows))
    scale = 1.0 / (16.0 * words * 4)
    groups = feeds // BLOCK
    chunks = words // LANES
    dma = pltpu.SemaphoreType.DMA
    vmem = pl.BlockSpec(memory_space=pltpu.VMEM)
    hbm = pl.BlockSpec(memory_space=pltpu.HBM)
    held = pl.pallas_call(
        functools.partial(gather_kernel, n, scale),
        out_shape=[
            pltpu.VMEM((2, feeds, feeds), jnp.float32),
            pltpu.VMEM((groups, 2 * BLOCK, 4 * words), PLANE),
            pltpu.VMEM((groups, 2 * BLOCK, 2 * BLOCK), jnp.float32),
            pltpu.VMEM((groups, BLOCK, 8), jnp.float32),
            pltpu.VMEM((groups, 2, BLOCK), jnp.float32),
        ],
        in_specs=[hbm] * 3,
        out_specs=[vmem] * 5,
        scratch_shapes=[
            pltpu.SMEM((1, slots), jnp.int32),
            pltpu.VMEM((2, slots, BLOCK), jnp.float32),
            pltpu.VMEM((slots, rows, words), jnp.int32),
            pltpu.VMEM((slots, rows, words), jnp.int32),
            pltpu.VMEM((slots, 2, BLOCK), jnp.float32),
            pltpu.VMEM((n, rows, words), jnp.int32),
            pltpu.VMEM((n, 2, BLOCK), jnp.float32),
            dma, dma, dma, dma((n, chunks)), dma((n, chunks)), dma((n,)), dma((n,)),
        ],
        compiler_params=pltpu.CompilerParams(
            collective_id=0, has_side_effects=True, vmem_limit_bytes=24 * 1024 * 1024),
    )(*[pltpu.with_memory_space_constraint(x, pltpu.HBM) for x in (channel_map, voltages, gains)])
    vis = pl.pallas_call(
        write_kernel,
        out_shape=jax.ShapeDtypeStruct((2, feeds, feeds), jnp.float32),
        in_specs=[vmem] * 5,
        out_specs=hbm,
        scratch_shapes=[
            pltpu.VMEM((groups, 2, BLOCK, BLOCK), jnp.float32),
            pltpu.VMEM((groups, 2, BLOCK, BLOCK), jnp.float32),
            dma((groups * groups,)),
        ],
        compiler_params=pltpu.CompilerParams(vmem_limit_bytes=16 * 1024 * 1024),
    )(*held)
    return vis[:, None, None]


def solution(mesh):
    in_specs = (P("band", None, "feed", None), P(None, "band", None, "feed"), P("band", None))
    out_specs = P(None, "band", "feed", None, None)
    return jax.shard_map(body, mesh=mesh, in_specs=in_specs, out_specs=out_specs, check_vma=False)
```

profile of v0, /device:TPU:0, one launch (start us, length us, event | category | flops | bytes accessed | tf_op | source)
XLA Modules:
  0.0 34.6 jit_solution(16680142860840539365)
XLA Ops:
  0.0 30.1 %shard_map.37 = (f32[2,1024,1024]{2,1,0:T(8,128)S(1)}, bf16[8,256,2048]{2,1,0:T(8,128)(2,1)S(1)}, f32[8,256,256]{2,1,0:T(8,128)S(1)}, f32[8,128,8]{2,1,0:T(8,128)S(1)}, f32[8,2,128]{2,1,0:T(2,128)S(1)}) custom-call(s32[1,8]{1,0:T(1,128)} %map_hbm.1, s32[1,8,128,512]{3,2,1,0:T(8,128)} %volt_hbm.1, f32[2,8,128]{2,1,0:T(8,128)} %bitcast.4), custom_call_target="tpu_custom_call" | custom-call | tf_op jit(solution)/shard_map/pallas_call | solution.py:228
  30.2 4.4 %shard_map.38 = f32[2,1024,1024]{2,1,0:T(8,128)} custom-call(f32[2,1024,1024]{2,1,0:T(8,128)S(1)} %get-tuple-element.10.vis_ref, bf16[8,256,2048]{2,1,0:T(8,128)(2,1)S(1)} %get-tuple-element.11.planes, f32[8,256,256]{2,1,0:T(8,128)S(1)} %get-tuple-element.12.acc, f32[8,128,8]{2,1,0:T(8,128)S(1)} %get-tuple-element.13.gcols, ...), custom_call_target="tpu_custom_call" | custom-call | tf_op jit(solution)/shard_map/pallas_call | solution.py:252
where the time goes:
time: 34.7 us; the launch traced here: 34.6 us
  Pallas kernels  34.6 us (100%)
    pallas_call x1, Pallas kernels, body(): pl.pallas_call(functools.partial(gather_kernel, n, scale), out_shape=[plt...  30.1 us
    pallas_call x1, Pallas kernels, body(): pl.pallas_call(write_kernel, out_shape=jax.ShapeDtypeStruct((2, feeds, fe...  4.44 us

commit v1 on v0

v1 whole, which is shorter than its diff:
```python
import functools

import jax
import jax.numpy as jnp
from jax import lax
from jax.experimental import pallas as pl
from jax.experimental.pallas import tpu as pltpu
from jax.sharding import PartitionSpec as P

MESH = pl.DeviceIdType.MESH
PLANE = jnp.bfloat16
BLOCK = 128
LANES = 128


def flip(index, mask, size):
    total, bit = 0, 1
    while bit < size:
        digit = lax.rem(index // bit, 2)
        total = total + ((1 - digit) if mask & bit else digit) * bit
        bit *= 2
    return total


def weigh(gram, col, row):
    gram_re = gram[:BLOCK, :BLOCK] + gram[BLOCK:, BLOCK:]
    gram_im = gram[BLOCK:, :BLOCK] - gram[:BLOCK, BLOCK:]
    col_re, col_im = col[:, 0:1], col[:, 1:2]
    row_re, row_im = row[0:1, :], row[1:2, :]
    weight_re = col_re * row_re + col_im * row_im
    weight_im = col_im * row_re - col_re * row_im
    return weight_re * gram_re - weight_im * gram_im, weight_re * gram_im + weight_im * gram_re


def product(left, right):
    return lax.dot_general(left, right, (((1,), (1,)), ((), ())), preferred_element_type=jnp.float32)


def send_order(n):
    return sorted(range(1, n), key=lambda m: (m & (m - 1) > 1 and bin(m >> 1).count("1") > 1, m & 1, m))


def group_order(n, per_group):
    seen = []
    for mask in [0] + send_order(n):
        if mask // per_group not in seen:
            seen.append(mask // per_group)
    return seen


def gather_kernel(n, scale, map_hbm, volt_hbm, gain_hbm, vis_ref, planes, acc, gcols, grows,
                  map_ref, gain_ref, volts, stage, gstage, recv, grecv,
                  map_sem, gain_sem, load_sem, send_sem, recv_sem, gsend_sem, grecv_sem):
    me = lax.axis_index("feed")
    rows, words = stage.shape[1], stage.shape[2]
    per_group = BLOCK // rows
    groups = n // per_group
    chunks = words // LANES
    low = lax.rem(me, per_group)
    own_group = me // per_group
    arrivals = group_order(n, per_group)
    whole, chunked = arrivals[:-2], arrivals[-2:]
    last = chunked[-1]
    pieces = len(volts)
    step = rows // pieces

    map_copy = pltpu.make_async_copy(map_hbm, map_ref, map_sem)
    gain_copy = pltpu.make_async_copy(gain_hbm, gain_ref, gain_sem)
    loads = []
    for p in range(pieces):
        strip = pl.ds(p * step, step)
        loads.append(pltpu.make_async_copy(volt_hbm.at[0, :, strip], volts[p], load_sem.at[p]))
    map_copy.start()
    for load in loads:
        load.start()
    gain_copy.start()
    barrier = pltpu.get_barrier_semaphore()
    for mask in range(1, n):
        pl.semaphore_signal(barrier, inc=1, device_id={"feed": flip(me, mask, n)}, device_id_type=MESH)
    map_copy.wait()
    order = send_order(n)
    lead, rest = order[:2], order[2:]
    copies = []

    def send(source, target, sent, landed, mask):
        copies.append(pltpu.make_async_remote_copy(
            src_ref=source, dst_ref=target, send_sem=sent, recv_sem=landed,
            device_id={"feed": flip(me, mask, n)}, device_id_type=MESH))
        copies[-1].start()

    def spot(mask):
        return (mask // per_group) * per_group + low

    for p in range(pieces):
        strip = pl.ds(p * step, step)
        loads[p].wait()
        for mask in lead:
            stage[mask, strip] = volts[p][map_ref[0, flip(me, mask, n)]]
        if p == 0:
            pl.semaphore_wait(barrier, n - 1)
        for mask in lead:
            send(stage.at[mask, strip], recv.at[spot(mask), strip], send_sem.at[mask, p],
                 recv_sem.at[spot(mask), p], mask)
    for mask in rest:
        for p in range(pieces):
            stage[mask, pl.ds(p * step, step)] = volts[p][map_ref[0, flip(me, mask, n)]]
        if mask // per_group in whole:
            send(stage.at[mask], recv.at[spot(mask)], send_sem.at[mask, 0], recv_sem.at[spot(mask), 0], mask)
    gain_copy.wait()
    for mask in range(n):
        channel = map_ref[0, flip(me, mask, n)]
        for part in range(2):
            gstage[mask, part:part + 1, :] = gain_ref[part, pl.ds(channel, 1), :]
    for mask in order:
        send(gstage.at[mask], grecv.at[spot(mask)], gsend_sem.at[mask], grecv_sem.at[spot(mask)], mask)
    for group in chunked:
        for c in range(chunks):
            part = pl.ds(c * LANES, LANES)
            for mask in rest:
                if mask // per_group == group:
                    send(stage.at[mask, :, part], recv.at[spot(mask), :, part], send_sem.at[mask, c],
                         recv_sem.at[spot(mask), c], mask)
    for p in range(pieces):
        recv[low, pl.ds(p * step, step)] = volts[p][map_ref[0, me]]
    grecv[low] = gstage[0]

    def places(group):
        return [group * per_group + flip(low, t, per_group) for t in range(per_group) if group or t]

    def arrive(group):
        for t in range(per_group):
            place = group * per_group + flip(low, t, per_group)
            if group * per_group + t in lead:
                for p in range(pieces):
                    here = recv.at[place, pl.ds(p * step, step)]
                    pltpu.make_async_copy(here, here, recv_sem.at[place, p]).wait()
            elif group or t:
                pltpu.make_async_copy(recv.at[place], recv.at[place], recv_sem.at[place, 0]).wait()

    def unpack(group, c):
        step = 32
        part_of = pl.ds(c * LANES, LANES)

        def piece(i, carry):
            start = pl.multiple_of(i * step, step)
            if rows >= step:
                packed = recv[group, pl.ds(start, step), part_of]
            else:
                first = group * per_group + i * (step // rows)
                packed = recv[pl.ds(first, step // rows), :, part_of].reshape(step, LANES)
            for k in range(4):
                for part in range(2):
                    field = jnp.right_shift(jnp.left_shift(packed, 28 - 8 * k - 4 * part), 28)
                    column = (4 * c + k) * LANES
                    planes[group, pl.ds(part * BLOCK + start, step), column:column + LANES] = (
                        field.astype(jnp.float32).astype(PLANE))
            return carry

        lax.fori_loop(0, BLOCK // step, piece, 0)

    def emit(group, other, gram):
        top = pl.multiple_of(flip(own_group, group, groups) * BLOCK, BLOCK)
        left = pl.multiple_of(flip(own_group, other, groups) * BLOCK, BLOCK)
        vis_re, vis_im = weigh(gram, gcols[group], grows[other])
        vis_ref[0, pl.ds(top, BLOCK), pl.ds(left, BLOCK)] = vis_re
        vis_ref[1, pl.ds(top, BLOCK), pl.ds(left, BLOCK)] = vis_im
        if other != group:
            vis_ref[0, pl.ds(left, BLOCK), pl.ds(top, BLOCK)] = jnp.transpose(vis_re)
            vis_ref[1, pl.ds(left, BLOCK), pl.ds(top, BLOCK)] = jnp.transpose(-vis_im)

    for group in range(groups):
        for place in places(group):
            pltpu.make_async_copy(grecv.at[place], grecv.at[place], grecv_sem.at[place]).wait()
        gains = grecv[group * per_group]
        for t in range(1, per_group):
            gains = gains + grecv[group * per_group + t]
        grows[group] = gains
        gcols[group] = jnp.transpose(jnp.concatenate([gains * scale] + [jnp.zeros_like(gains)] * 3, axis=0))

    for position, group in enumerate(whole):
        arrive(group)
        for c in range(chunks):
            unpack(group, c)
        for other in whole[:position + 1]:
            emit(group, other, product(planes[group], planes[other]))

    for group in chunked:
        others = arrivals[:arrivals.index(group) + 1]
        for c in range(chunks):
            for place in places(group):
                here = recv.at[place, :, pl.ds(c * LANES, LANES)]
                pltpu.make_async_copy(here, here, recv_sem.at[place, c]).wait()
            unpack(group, c)
            span = pl.ds(4 * c * LANES, 4 * LANES)
            if c < chunks - 1 or group != last:
                for other in others:
                    term = product(planes[group, :, span], planes[other, :, span])
                    gram = term if c == 0 else acc[other] + term
                    if c < chunks - 1:
                        acc[other] = gram
                    else:
                        emit(group, other, gram)

    for copy in copies:
        copy.wait_send()


def write_kernel(vis_ref, planes, acc, gcols, grows, out_hbm, gram, row_strip, column_strip, sems):
    groups = planes.shape[0]
    per_group = lax.axis_size("feed") // groups
    own_group = lax.axis_index("feed") // per_group
    last = group_order(lax.axis_size("feed"), per_group)[-1]
    span = pl.ds(planes.shape[2] - 4 * LANES, 4 * LANES)

    def spot(group):
        return pl.ds(pl.multiple_of(flip(own_group, group, groups) * BLOCK, BLOCK), BLOCK)

    copies = []

    def write(source, rows, columns):
        copies.append(pltpu.make_async_copy(source, out_hbm.at[:, rows, columns], sems.at[len(copies)]))
        copies[-1].start()

    for group in range(groups):
        if group == last:
            continue
        size = groups // 2
        while size:
            prefix = last // size * size ^ size
            start = flip(own_group, prefix, groups) // size * size
            columns = pl.ds(pl.multiple_of(start * BLOCK, BLOCK), size * BLOCK)
            write(vis_ref.at[:, spot(group), columns], spot(group), columns)
            size //= 2
    for other in range(groups):
        gram[other] = acc[other] + product(planes[last, :, span], planes[other, :, span])
    for other in range(groups):
        vis_re, vis_im = weigh(gram[other], gcols[last], grows[other])
        row_strip[other, 0] = vis_re
        row_strip[other, 1] = vis_im
        write(row_strip.at[other], spot(last), spot(other))
        if other != last:
            column_strip[other, 0] = jnp.transpose(vis_re)
            column_strip[other, 1] = jnp.transpose(-vis_im)
            write(column_strip.at[other], spot(other), spot(last))
    for copy in copies:
        copy.wait()


def body(voltages, complex_gains, channel_map):
    n = lax.axis_size("feed")
    slots, rows, words = voltages.shape[1:]
    feeds = rows * n
    gains = complex_gains[:, 0]
    per_group = BLOCK // rows
    if per_group > 1:
        low = lax.rem(lax.axis_index("feed"), per_group)
        gains = lax.dynamic_update_slice(jnp.zeros((2, slots, BLOCK), gains.dtype), gains, (0, 0, low * rows))
    scale = 1.0 / (16.0 * words * 4)
    groups = feeds // BLOCK
    chunks = words // LANES
    pieces = 4 if rows % 32 == 0 else 1
    slices = max(chunks, pieces)
    dma = pltpu.SemaphoreType.DMA
    vmem = pl.BlockSpec(memory_space=pltpu.VMEM)
    hbm = pl.BlockSpec(memory_space=pltpu.HBM)
    held = pl.pallas_call(
        functools.partial(gather_kernel, n, scale),
        out_shape=[
            pltpu.VMEM((2, feeds, feeds), jnp.float32),
            pltpu.VMEM((groups, 2 * BLOCK, 4 * words), PLANE),
            pltpu.VMEM((groups, 2 * BLOCK, 2 * BLOCK), jnp.float32),
            pltpu.VMEM((groups, BLOCK, 8), jnp.float32),
            pltpu.VMEM((groups, 2, BLOCK), jnp.float32),
        ],
        in_specs=[hbm] * 3,
        out_specs=[vmem] * 5,
        scratch_shapes=[
            pltpu.SMEM((1, slots), jnp.int32),
            pltpu.VMEM((2, slots, BLOCK), jnp.float32),
            [pltpu.VMEM((slots, rows // pieces, words), jnp.int32)] * pieces,
            pltpu.VMEM((slots, rows, words), jnp.int32),
            pltpu.VMEM((slots, 2, BLOCK), jnp.float32),
            pltpu.VMEM((n, rows, words), jnp.int32),
            pltpu.VMEM((n, 2, BLOCK), jnp.float32),
            dma, dma, dma((pieces,)), dma((n, slices)), dma((n, slices)), dma((n,)), dma((n,)),
        ],
        compiler_params=pltpu.CompilerParams(
            collective_id=0, has_side_effects=True, vmem_limit_bytes=24 * 1024 * 1024),
    )(*[pltpu.with_memory_space_constraint(x, pltpu.HBM) for x in (channel_map, voltages, gains)])
    vis = pl.pallas_call(
        write_kernel,
        out_shape=jax.ShapeDtypeStruct((2, feeds, feeds), jnp.float32),
        in_specs=[vmem] * 5,
        out_specs=hbm,
        scratch_shapes=[
            pltpu.VMEM((groups, 2 * BLOCK, 2 * BLOCK), jnp.float32),
            pltpu.VMEM((groups, 2, BLOCK, BLOCK), jnp.float32),
            pltpu.VMEM((groups, 2, BLOCK, BLOCK), jnp.float32),
            dma((groups * groups,)),
        ],
        compiler_params=pltpu.CompilerParams(vmem_limit_bytes=16 * 1024 * 1024),
    )(*held)
    return vis[:, None, None]


def solution(mesh):
    in_specs = (P("band", None, "feed", None), P(None, "band", None, "feed"), P("band", None))
    out_specs = P(None, "band", "feed", None, None)
    return jax.shard_map(body, mesh=mesh, in_specs=in_specs, out_specs=out_specs, check_vma=False)
```

time: 34.7 us -> 41.8 us (1.20)
  Pallas kernels: 34.6 us -> 41.6 us
    pallas_call x1, Pallas kernels: 30.1 us -> 37.8 us  [body(): pl.pallas_call(functools.partial(gather_kernel, n, scale), out_shape=[plt...]
    pallas_call x1, Pallas kernels: 4.44 us -> 3.85 us  [body(): pl.pallas_call(write_kernel, out_shape=jax.ShapeDtypeStruct((2, feeds, fe...]
where the time goes in v1:
time: 41.8 us; the launch traced here: 41.7 us
  Pallas kernels  41.6 us (100%)
    pallas_call x1, Pallas kernels, body(): pl.pallas_call(functools.partial(gather_kernel, n, scale), out_shape=[plt...  37.8 us
    pallas_call x1, Pallas kernels, body(): pl.pallas_call(write_kernel, out_shape=jax.ShapeDtypeStruct((2, feeds, fe...  3.85 us

profile of v1, /device:TPU:0, one launch (start us, length us, event | category | flops | bytes accessed | tf_op | source)
XLA Modules:
  0.0 41.7 jit_solution(15395017615364648813)
XLA Ops:
  0.0 37.8 %shard_map.37 = (f32[2,1024,1024]{2,1,0:T(8,128)S(1)}, bf16[8,256,2048]{2,1,0:T(8,128)(2,1)S(1)}, f32[8,256,256]{2,1,0:T(8,128)S(1)}, f32[8,128,8]{2,1,0:T(8,128)S(1)}, f32[8,2,128]{2,1,0:T(2,128)S(1)}) custom-call(s32[1,8]{1,0:T(1,128)} %map_hbm.1, s32[1,8,128,512]{3,2,1,0:T(8,128)} %volt_hbm.1, f32[2,8,128]{2,1,0:T(8,128)} %bitcast.4), custom_call_target="tpu_custom_call" | custom-call | tf_op jit(solution)/shard_map/pallas_call | solution.py:266
  37.8 3.9 %shard_map.38 = f32[2,1024,1024]{2,1,0:T(8,128)} custom-call(f32[2,1024,1024]{2,1,0:T(8,128)S(1)} %get-tuple-element.10.vis_ref, bf16[8,256,2048]{2,1,0:T(8,128)(2,1)S(1)} %get-tuple-element.11.planes, f32[8,256,256]{2,1,0:T(8,128)S(1)} %get-tuple-element.12.acc, f32[8,128,8]{2,1,0:T(8,128)S(1)} %get-tuple-element.13.gcols, ...), custom_call_target="tpu_custom_call" | custom-call | tf_op jit(solution)/shard_map/pallas_call | solution.py:290

commit v2 on v1

--- a/solution.py
+++ b/solution.py
@@ -101,18 +101,19 @@
         for mask in lead:
             send(stage.at[mask, strip], recv.at[spot(mask), strip], send_sem.at[mask, p],
                  recv_sem.at[spot(mask), p], mask)
+        if p == 0:
+            gain_copy.wait()
+            for mask in range(n):
+                channel = map_ref[0, flip(me, mask, n)]
+                for part in range(2):
+                    gstage[mask, part:part + 1, :] = gain_ref[part, pl.ds(channel, 1), :]
+            for mask in order:
+                send(gstage.at[mask], grecv.at[spot(mask)], gsend_sem.at[mask], grecv_sem.at[spot(mask)], mask)
     for mask in rest:
         for p in range(pieces):
             stage[mask, pl.ds(p * step, step)] = volts[p][map_ref[0, flip(me, mask, n)]]
         if mask // per_group in whole:
             send(stage.at[mask], recv.at[spot(mask)], send_sem.at[mask, 0], recv_sem.at[spot(mask), 0], mask)
-    gain_copy.wait()
-    for mask in range(n):
-        channel = map_ref[0, flip(me, mask, n)]
-        for part in range(2):
-            gstage[mask, part:part + 1, :] = gain_ref[part, pl.ds(channel, 1), :]
-    for mask in order:
-        send(gstage.at[mask], grecv.at[spot(mask)], gsend_sem.at[mask], grecv_sem.at[spot(mask)], mask)
     for group in chunked:
         for c in range(chunks):
             part = pl.ds(c * LANES, LANES)

time: 41.8 us -> 34.4 us (0.82)
  Pallas kernels: 41.6 us -> 34.2 us
    pallas_call x1, Pallas kernels: 37.8 us -> 30.4 us  [body(): pl.pallas_call(functools.partial(gather_kernel, n, scale), out_shape=[plt...]
where the time goes in v2:
time: 34.4 us; the launch traced here: 34.2 us
  Pallas kernels  34.2 us (99%)
    pallas_call x1, Pallas kernels, body(): pl.pallas_call(functools.partial(gather_kernel, n, scale), out_shape=[plt...  30.4 us
    pallas_call x1, Pallas kernels, body(): pl.pallas_call(write_kernel, out_shape=jax.ShapeDtypeStruct((2, feeds, fe...  3.85 us

profile of v2, /device:TPU:0, one launch (start us, length us, event | category | flops | bytes accessed | tf_op | source)
XLA Modules:
  0.0 34.2 jit_solution(4587332698067156971)
XLA Ops:
  0.0 30.4 %shard_map.37 = (f32[2,1024,1024]{2,1,0:T(8,128)S(1)}, bf16[8,256,2048]{2,1,0:T(8,128)(2,1)S(1)}, f32[8,256,256]{2,1,0:T(8,128)S(1)}, f32[8,128,8]{2,1,0:T(8,128)S(1)}, f32[8,2,128]{2,1,0:T(2,128)S(1)}) custom-call(s32[1,8]{1,0:T(1,128)} %map_hbm.1, s32[1,8,128,512]{3,2,1,0:T(8,128)} %volt_hbm.1, f32[2,8,128]{2,1,0:T(8,128)} %bitcast.4), custom_call_target="tpu_custom_call" | custom-call | tf_op jit(solution)/shard_map/pallas_call | solution.py:267
  30.4 3.9 %shard_map.38 = f32[2,1024,1024]{2,1,0:T(8,128)} custom-call(f32[2,1024,1024]{2,1,0:T(8,128)S(1)} %get-tuple-element.10.vis_ref, bf16[8,256,2048]{2,1,0:T(8,128)(2,1)S(1)} %get-tuple-element.11.planes, f32[8,256,256]{2,1,0:T(8,128)S(1)} %get-tuple-element.12.acc, f32[8,128,8]{2,1,0:T(8,128)S(1)} %get-tuple-element.13.gcols, ...), custom_call_target="tpu_custom_call" | custom-call | tf_op jit(solution)/shard_map/pallas_call | solution.py:291

commit v3 on v2

--- a/solution.py
+++ b/solution.py
@@ -11,6 +11,7 @@
 PLANE = jnp.bfloat16
 BLOCK = 128
 LANES = 128
+TAIL = 3
 
 
 def flip(index, mask, size):
@@ -185,6 +186,7 @@
         for other in whole[:position + 1]:
             emit(group, other, product(planes[group], planes[other]))
 
+    pair = max(chunks // 2, 1)
     for group in chunked:
         others = arrivals[:arrivals.index(group) + 1]
         for c in range(chunks):
@@ -192,11 +194,17 @@
                 here = recv.at[place, :, pl.ds(c * LANES, LANES)]
                 pltpu.make_async_copy(here, here, recv_sem.at[place, c]).wait()
             unpack(group, c)
-            span = pl.ds(4 * c * LANES, 4 * LANES)
-            if c < chunks - 1 or group != last:
+            if group == last:
+                span = pl.ds(4 * c * LANES, 4 * LANES)
+                if c < chunks - TAIL:
+                    for other in others:
+                        term = product(planes[group, :, span], planes[other, :, span])
+                        acc[other] = term if c == 0 else acc[other] + term
+            elif (c + 1) % pair == 0:
+                span = pl.ds(4 * (c + 1 - pair) * LANES, 4 * pair * LANES)
                 for other in others:
                     term = product(planes[group, :, span], planes[other, :, span])
-                    gram = term if c == 0 else acc[other] + term
+                    gram = term if c + 1 == pair else acc[other] + term
                     if c < chunks - 1:
                         acc[other] = gram
                     else:
@@ -211,7 +219,7 @@
     per_group = lax.axis_size("feed") // groups
     own_group = lax.axis_index("feed") // per_group
     last = group_order(lax.axis_size("feed"), per_group)[-1]
-    span = pl.ds(planes.shape[2] - 4 * LANES, 4 * LANES)
+    span = pl.ds(planes.shape[2] - 4 * TAIL * LANES, 4 * TAIL * LANES)
 
     def spot(group):
         return pl.ds(pl.multiple_of(flip(own_group, group, groups) * BLOCK, BLOCK), BLOCK)

time: 34.4 us -> 32.8 us (0.953)
  Pallas kernels: 34.2 us -> 32.3 us
    pallas_call x1, Pallas kernels: 30.4 us -> 28.4 us  [body(): pl.pallas_call(functools.partial(gather_kernel, n, scale), out_shape=[plt...]
where the time goes in v3:
time: 32.8 us; the launch traced here: 32.5 us
  Pallas kernels  32.3 us (98%)
    pallas_call x1, Pallas kernels, body(): pl.pallas_call(functools.partial(gather_kernel, n, scale), out_shape=[plt...  28.4 us
    pallas_call x1, Pallas kernels, body(): pl.pallas_call(write_kernel, out_shape=jax.ShapeDtypeStruct((2, feeds, fe...  3.85 us

profile of v3, /device:TPU:0, one launch (start us, length us, event | category | flops | bytes accessed | tf_op | source)
XLA Modules:
  0.0 32.5 jit_solution(14915781791522274369)
XLA Ops:
  0.0 28.4 %shard_map.37 = (f32[2,1024,1024]{2,1,0:T(8,128)S(1)}, bf16[8,256,2048]{2,1,0:T(8,128)(2,1)S(1)}, f32[8,256,256]{2,1,0:T(8,128)S(1)}, f32[8,128,8]{2,1,0:T(8,128)S(1)}, f32[8,2,128]{2,1,0:T(2,128)S(1)}) custom-call(s32[1,8]{1,0:T(1,128)} %map_hbm.1, s32[1,8,128,512]{3,2,1,0:T(8,128)} %volt_hbm.1, f32[2,8,128]{2,1,0:T(8,128)} %bitcast.4), custom_call_target="tpu_custom_call" | custom-call | tf_op jit(solution)/shard_map/pallas_call | solution.py:275
  28.5 3.9 %shard_map.38 = f32[2,1024,1024]{2,1,0:T(8,128)} custom-call(f32[2,1024,1024]{2,1,0:T(8,128)S(1)} %get-tuple-element.10.vis_ref, bf16[8,256,2048]{2,1,0:T(8,128)(2,1)S(1)} %get-tuple-element.11.planes, f32[8,256,256]{2,1,0:T(8,128)S(1)} %get-tuple-element.12.acc, f32[8,128,8]{2,1,0:T(8,128)S(1)} %get-tuple-element.13.gcols, ...), custom_call_target="tpu_custom_call" | custom-call | tf_op jit(solution)/shard_map/pallas_call | solution.py:299

commit v4 on v2

--- a/solution.py
+++ b/solution.py
@@ -11,6 +11,7 @@
 PLANE = jnp.bfloat16
 BLOCK = 128
 LANES = 128
+TAIL = 3
 
 
 def flip(index, mask, size):
@@ -50,7 +51,7 @@
 
 def gather_kernel(n, scale, map_hbm, volt_hbm, gain_hbm, vis_ref, planes, acc, gcols, grows,
                   map_ref, gain_ref, volts, stage, gstage, recv, grecv,
-                  map_sem, gain_sem, load_sem, send_sem, recv_sem, gsend_sem, grecv_sem):
+                  map_sem, gain_sem, load_sem, send_sem, whole_sem, half_sem, last_sem, gsend_sem, grecv_sem):
     me = lax.axis_index("feed")
     rows, words = stage.shape[1], stage.shape[2]
     per_group = BLOCK // rows
@@ -80,13 +81,20 @@
     map_copy.wait()
     order = send_order(n)
     lead, rest = order[:2], order[2:]
-    copies = []
+    pair = max(chunks // 2, 1)
 
     def send(source, target, sent, landed, mask):
-        copies.append(pltpu.make_async_remote_copy(
+        pltpu.make_async_remote_copy(
             src_ref=source, dst_ref=target, send_sem=sent, recv_sem=landed,
-            device_id={"feed": flip(me, mask, n)}, device_id_type=MESH))
-        copies[-1].start()
+            device_id={"feed": flip(me, mask, n)}, device_id_type=MESH).start()
+
+    def landing(group, place, c):
+        inner = place - group * per_group
+        if group == last:
+            return last_sem.at[inner, c]
+        if group in chunked:
+            return half_sem.at[inner, c // pair]
+        return whole_sem.at[whole.index(group) * per_group + inner]
 
     def spot(mask):
         return (mask // per_group) * per_group + low
@@ -99,8 +107,8 @@
         if p == 0:
             pl.semaphore_wait(barrier, n - 1)
         for mask in lead:
-            send(stage.at[mask, strip], recv.at[spot(mask), strip], send_sem.at[mask, p],
-                 recv_sem.at[spot(mask), p], mask)
+            send(stage.at[mask, strip], recv.at[spot(mask), strip], send_sem,
+                 landing(mask // per_group, spot(mask), 0), mask)
         if p == 0:
             gain_copy.wait()
             for mask in range(n):
@@ -108,19 +116,19 @@
                 for part in range(2):
                     gstage[mask, part:part + 1, :] = gain_ref[part, pl.ds(channel, 1), :]
             for mask in order:
-                send(gstage.at[mask], grecv.at[spot(mask)], gsend_sem.at[mask], grecv_sem.at[spot(mask)], mask)
+                send(gstage.at[mask], grecv.at[spot(mask)], gsend_sem, grecv_sem, mask)
     for mask in rest:
         for p in range(pieces):
             stage[mask, pl.ds(p * step, step)] = volts[p][map_ref[0, flip(me, mask, n)]]
         if mask // per_group in whole:
-            send(stage.at[mask], recv.at[spot(mask)], send_sem.at[mask, 0], recv_sem.at[spot(mask), 0], mask)
+            send(stage.at[mask], recv.at[spot(mask)], send_sem, landing(mask // per_group, spot(mask), 0), mask)
     for group in chunked:
         for c in range(chunks):
             part = pl.ds(c * LANES, LANES)
             for mask in rest:
                 if mask // per_group == group:
-                    send(stage.at[mask, :, part], recv.at[spot(mask), :, part], send_sem.at[mask, c],
-                         recv_sem.at[spot(mask), c], mask)
+                    send(stage.at[mask, :, part], recv.at[spot(mask), :, part], send_sem,
+                         landing(group, spot(mask), c), mask)
     for p in range(pieces):
         recv[low, pl.ds(p * step, step)] = volts[p][map_ref[0, me]]
     grecv[low] = gstage[0]
@@ -129,14 +137,8 @@
         return [group * per_group + flip(low, t, per_group) for t in range(per_group) if group or t]
 
     def arrive(group):
-        for t in range(per_group):
-            place = group * per_group + flip(low, t, per_group)
-            if group * per_group + t in lead:
-                for p in range(pieces):
-                    here = recv.at[place, pl.ds(p * step, step)]
-                    pltpu.make_async_copy(here, here, recv_sem.at[place, p]).wait()
-            elif group or t:
-                pltpu.make_async_copy(recv.at[place], recv.at[place], recv_sem.at[place, 0]).wait()
+        for place in places(group):
+            pltpu.make_async_copy(recv.at[place], recv.at[place], landing(group, place, 0)).wait()
 
     def unpack(group, c):
         step = 32
@@ -169,9 +171,8 @@
             vis_ref[0, pl.ds(left, BLOCK), pl.ds(top, BLOCK)] = jnp.transpose(vis_re)
             vis_ref[1, pl.ds(left, BLOCK), pl.ds(top, BLOCK)] = jnp.transpose(-vis_im)
 
+    pltpu.make_async_copy(gstage.at[pl.ds(1, n - 1)], grecv.at[pl.ds(1, n - 1)], grecv_sem).wait()
     for group in range(groups):
-        for place in places(group):
-            pltpu.make_async_copy(grecv.at[place], grecv.at[place], grecv_sem.at[place]).wait()
         gains = grecv[group * per_group]
         for t in range(1, per_group):
             gains = gains + grecv[group * per_group + t]
@@ -185,42 +186,51 @@
         for other in whole[:position + 1]:
             emit(group, other, product(planes[group], planes[other]))
 
-    for group in chunked:
-        others = arrivals[:arrivals.index(group) + 1]
-        for c in range(chunks):
-            for place in places(group):
-                here = recv.at[place, :, pl.ds(c * LANES, LANES)]
-                pltpu.make_async_copy(here, here, recv_sem.at[place, c]).wait()
-            unpack(group, c)
-            span = pl.ds(4 * c * LANES, 4 * LANES)
-            if c < chunks - 1 or group != last:
-                for other in others:
-                    term = product(planes[group, :, span], planes[other, :, span])
-                    gram = term if c == 0 else acc[other] + term
-                    if c < chunks - 1:
-                        acc[other] = gram
-                    else:
-                        emit(group, other, gram)
-
-    for copy in copies:
-        copy.wait_send()
-
-
-def write_kernel(vis_ref, planes, acc, gcols, grows, out_hbm, gram, row_strip, column_strip, sems):
+    halved = chunked[0]
+    others = arrivals[:-1]
+    for h in range(chunks // pair):
+        part = pl.ds(h * pair * LANES, pair * LANES)
+        for place in places(halved):
+            here = recv.at[place, :, part]
+            pltpu.make_async_copy(here, here, landing(halved, place, h * pair)).wait()
+        for c in range(h * pair, (h + 1) * pair):
+            unpack(halved, c)
+        span = pl.ds(4 * h * pair * LANES, 4 * pair * LANES)
+        for other in others:
+            term = product(planes[halved, :, span], planes[other, :, span])
+            gram = term if h == 0 else acc[other] + term
+            if h < chunks // pair - 1:
+                acc[other] = gram
+            else:
+                emit(halved, other, gram)
+
+    for c in range(chunks):
+        for place in places(last):
+            here = recv.at[place, :, pl.ds(c * LANES, LANES)]
+            pltpu.make_async_copy(here, here, landing(last, place, c)).wait()
+        unpack(last, c)
+        span = pl.ds(4 * c * LANES, 4 * LANES)
+        if c < chunks - TAIL:
+            for other in arrivals:
+                term = product(planes[last, :, span], planes[other, :, span])
+                acc[other] = term if c == 0 else acc[other] + term
+
+    pltpu.make_async_copy(stage.at[pl.ds(1, n - 1)], recv.at[pl.ds(1, n - 1)], send_sem).wait()
+    pltpu.make_async_copy(gstage.at[pl.ds(1, n - 1)], grecv.at[pl.ds(1, n - 1)], gsend_sem).wait()
+
+
+def write_kernel(vis_ref, planes, acc, gcols, grows, out_hbm, gram, row_strip, column_strip, sem):
     groups = planes.shape[0]
     per_group = lax.axis_size("feed") // groups
     own_group = lax.axis_index("feed") // per_group
     last = group_order(lax.axis_size("feed"), per_group)[-1]
-    span = pl.ds(planes.shape[2] - 4 * LANES, 4 * LANES)
+    span = pl.ds(planes.shape[2] - 4 * TAIL * LANES, 4 * TAIL * LANES)
 
     def spot(group):
         return pl.ds(pl.multiple_of(flip(own_group, group, groups) * BLOCK, BLOCK), BLOCK)
 
-    copies = []
-
     def write(source, rows, columns):
-        copies.append(pltpu.make_async_copy(source, out_hbm.at[:, rows, columns], sems.at[len(copies)]))
-        copies[-1].start()
+        pltpu.make_async_copy(source, out_hbm.at[:, rows, columns], sem).start()
 
     for group in range(groups):
         if group == last:
@@ -243,8 +253,7 @@
             column_strip[other, 0] = jnp.transpose(vis_re)
             column_strip[other, 1] = jnp.transpose(-vis_im)
             write(column_strip.at[other], spot(other), spot(last))
-    for copy in copies:
-        copy.wait()
+    pltpu.make_async_copy(vis_ref, out_hbm, sem).wait()
 
 
 def body(voltages, complex_gains, channel_map):
@@ -260,7 +269,6 @@
     groups = feeds // BLOCK
     chunks = words // LANES
     pieces = 4 if rows % 32 == 0 else 1
-    slices = max(chunks, pieces)
     dma = pltpu.SemaphoreType.DMA
     vmem = pl.BlockSpec(memory_space=pltpu.VMEM)
     hbm = pl.BlockSpec(memory_space=pltpu.HBM)
@@ -283,7 +291,8 @@
             pltpu.VMEM((slots, 2, BLOCK), jnp.float32),
             pltpu.VMEM((n, rows, words), jnp.int32),
             pltpu.VMEM((n, 2, BLOCK), jnp.float32),
-            dma, dma, dma((pieces,)), dma((n, slices)), dma((n, slices)), dma((n,)), dma((n,)),
+            dma, dma, dma((pieces,)), dma, dma((n - 2 * per_group,)), dma((per_group, 2)),
+            dma((per_group, chunks)), dma, dma,
         ],
         compiler_params=pltpu.CompilerParams(
             collective_id=0, has_side_effects=True, vmem_limit_bytes=24 * 1024 * 1024),
@@ -297,7 +306,7 @@
             pltpu.VMEM((groups, 2 * BLOCK, 2 * BLOCK), jnp.float32),
             pltpu.VMEM((groups, 2, BLOCK, BLOCK), jnp.float32),
             pltpu.VMEM((groups, 2, BLOCK, BLOCK), jnp.float32),
-            dma((groups * groups,)),
+            dma,
         ],
         compiler_params=pltpu.CompilerParams(vmem_limit_bytes=16 * 1024 * 1024),
     )(*held)

time: 34.4 us -> 31.3 us (0.910)
  Pallas kernels: 34.2 us -> 30.9 us
    pallas_call x1, Pallas kernels: 30.4 us -> 27.6 us  [body(): pl.pallas_call(functools.partial(gather_kernel, n, scale), out_shape=[plt...]
    pallas_call x1, Pallas kernels: 3.85 us -> 3.29 us  [body(): pl.pallas_call(write_kernel, out_shape=jax.ShapeDtypeStruct((2, feeds, fe...]
where the time goes in v4:
time: 31.3 us; the launch traced here: 30.9 us
  Pallas kernels  30.9 us (99%)
    pallas_call x1, Pallas kernels, body(): pl.pallas_call(functools.partial(gather_kernel, n, scale), out_shape=[plt...  27.6 us
    pallas_call x1, Pallas kernels, body(): pl.pallas_call(write_kernel, out_shape=jax.ShapeDtypeStruct((2, feeds, fe...  3.29 us

profile of v4, /device:TPU:0, one launch (start us, length us, event | category | flops | bytes accessed | tf_op | source)
XLA Modules:
  0.0 30.9 jit_solution(12159657655671458646)
XLA Ops:
  0.0 27.6 %shard_map.37 = (f32[2,1024,1024]{2,1,0:T(8,128)S(1)}, bf16[8,256,2048]{2,1,0:T(8,128)(2,1)S(1)}, f32[8,256,256]{2,1,0:T(8,128)S(1)}, f32[8,128,8]{2,1,0:T(8,128)S(1)}, f32[8,2,128]{2,1,0:T(2,128)S(1)}) custom-call(s32[1,8]{1,0:T(1,128)} %map_hbm.1, s32[1,8,128,512]{3,2,1,0:T(8,128)} %volt_hbm.1, f32[2,8,128]{2,1,0:T(8,128)} %bitcast.4), custom_call_target="tpu_custom_call" | custom-call | tf_op jit(solution)/shard_map/pallas_call | solution.py:275
  27.7 3.3 %shard_map.38 = f32[2,1024,1024]{2,1,0:T(8,128)} custom-call(f32[2,1024,1024]{2,1,0:T(8,128)S(1)} %get-tuple-element.10.vis_ref, bf16[8,256,2048]{2,1,0:T(8,128)(2,1)S(1)} %get-tuple-element.11.planes, f32[8,256,256]{2,1,0:T(8,128)S(1)} %get-tuple-element.12.acc, f32[8,128,8]{2,1,0:T(8,128)S(1)} %get-tuple-element.13.gcols, ...), custom_call_target="tpu_custom_call" | custom-call | tf_op jit(solution)/shard_map/pallas_call | solution.py:300

commit v5 on v4

--- a/solution.py
+++ b/solution.py
@@ -11,7 +11,16 @@
 PLANE = jnp.bfloat16
 BLOCK = 128
 LANES = 128
-TAIL = 3
+TAIL = 2
+
+
+def load_cuts(rows):
+    return [0, rows // 8, rows // 2, rows] if rows % 64 == 0 else [0, rows]
+
+
+def unpack_field(packed, k, part):
+    field = jnp.right_shift(jnp.left_shift(packed, 28 - 8 * k - 4 * part), 28)
+    return field.astype(jnp.float32).astype(PLANE)
 
 
 def flip(index, mask, size):
@@ -49,7 +58,7 @@
     return seen
 
 
-def gather_kernel(n, scale, map_hbm, volt_hbm, gain_hbm, vis_ref, planes, acc, gcols, grows,
+def gather_kernel(n, scale, map_hbm, volt_hbm, gain_hbm, vis_ref, planes, acc, gcols, grows, held,
                   map_ref, gain_ref, volts, stage, gstage, recv, grecv,
                   map_sem, gain_sem, load_sem, send_sem, whole_sem, half_sem, last_sem, gsend_sem, grecv_sem):
     me = lax.axis_index("feed")
@@ -62,22 +71,21 @@
     arrivals = group_order(n, per_group)
     whole, chunked = arrivals[:-2], arrivals[-2:]
     last = chunked[-1]
-    pieces = len(volts)
-    step = rows // pieces
+    cuts = load_cuts(rows)
+    strips = [pl.ds(a, b - a) for a, b in zip(cuts, cuts[1:])]
 
     map_copy = pltpu.make_async_copy(map_hbm, map_ref, map_sem)
     gain_copy = pltpu.make_async_copy(gain_hbm, gain_ref, gain_sem)
-    loads = []
-    for p in range(pieces):
-        strip = pl.ds(p * step, step)
-        loads.append(pltpu.make_async_copy(volt_hbm.at[0, :, strip], volts[p], load_sem.at[p]))
+    loads = [pltpu.make_async_copy(volt_hbm.at[0, :, strip], volts[p], load_sem.at[p])
+             for p, strip in enumerate(strips)]
+    loads[0].start()
     map_copy.start()
-    for load in loads:
-        load.start()
-    gain_copy.start()
     barrier = pltpu.get_barrier_semaphore()
     for mask in range(1, n):
         pl.semaphore_signal(barrier, inc=1, device_id={"feed": flip(me, mask, n)}, device_id_type=MESH)
+    for load in loads[1:]:
+        load.start()
+    gain_copy.start()
     map_copy.wait()
     order = send_order(n)
     lead, rest = order[:2], order[2:]
@@ -99,8 +107,7 @@
     def spot(mask):
         return (mask // per_group) * per_group + low
 
-    for p in range(pieces):
-        strip = pl.ds(p * step, step)
+    for p, strip in enumerate(strips):
         loads[p].wait()
         for mask in lead:
             stage[mask, strip] = volts[p][map_ref[0, flip(me, mask, n)]]
@@ -118,8 +125,8 @@
             for mask in order:
                 send(gstage.at[mask], grecv.at[spot(mask)], gsend_sem, grecv_sem, mask)
     for mask in rest:
-        for p in range(pieces):
-            stage[mask, pl.ds(p * step, step)] = volts[p][map_ref[0, flip(me, mask, n)]]
+        for p, strip in enumerate(strips):
+            stage[mask, strip] = volts[p][map_ref[0, flip(me, mask, n)]]
         if mask // per_group in whole:
             send(stage.at[mask], recv.at[spot(mask)], send_sem, landing(mask // per_group, spot(mask), 0), mask)
     for group in chunked:
@@ -129,8 +136,8 @@
                 if mask // per_group == group:
                     send(stage.at[mask, :, part], recv.at[spot(mask), :, part], send_sem,
                          landing(group, spot(mask), c), mask)
-    for p in range(pieces):
-        recv[low, pl.ds(p * step, step)] = volts[p][map_ref[0, me]]
+    for p, strip in enumerate(strips):
+        recv[low, strip] = volts[p][map_ref[0, me]]
     grecv[low] = gstage[0]
 
     def places(group):
@@ -153,10 +160,9 @@
                 packed = recv[pl.ds(first, step // rows), :, part_of].reshape(step, LANES)
             for k in range(4):
                 for part in range(2):
-                    field = jnp.right_shift(jnp.left_shift(packed, 28 - 8 * k - 4 * part), 28)
                     column = (4 * c + k) * LANES
                     planes[group, pl.ds(part * BLOCK + start, step), column:column + LANES] = (
-                        field.astype(jnp.float32).astype(PLANE))
+                        unpack_field(packed, k, part))
             return carry
 
         lax.fori_loop(0, BLOCK // step, piece, 0)
@@ -208,6 +214,9 @@
         for place in places(last):
             here = recv.at[place, :, pl.ds(c * LANES, LANES)]
             pltpu.make_async_copy(here, here, landing(last, place, c)).wait()
+        if c == chunks - 1:
+            held[...] = recv[pl.ds(last * per_group, per_group), :, pl.ds(c * LANES, LANES)].reshape(BLOCK, LANES)
+            break
         unpack(last, c)
         span = pl.ds(4 * c * LANES, 4 * LANES)
         if c < chunks - TAIL:
@@ -219,12 +228,14 @@
     pltpu.make_async_copy(gstage.at[pl.ds(1, n - 1)], grecv.at[pl.ds(1, n - 1)], gsend_sem).wait()
 
 
-def write_kernel(vis_ref, planes, acc, gcols, grows, out_hbm, gram, row_strip, column_strip, sem):
+def write_kernel(vis_ref, planes, acc, gcols, grows, held, out_hbm, tail, gram, row_strip, column_strip, sem):
     groups = planes.shape[0]
     per_group = lax.axis_size("feed") // groups
     own_group = lax.axis_index("feed") // per_group
     last = group_order(lax.axis_size("feed"), per_group)[-1]
-    span = pl.ds(planes.shape[2] - 4 * TAIL * LANES, 4 * TAIL * LANES)
+    chunks = planes.shape[2] // (4 * LANES)
+    middle = pl.ds(4 * max(chunks - TAIL, 0) * LANES, 4 * (min(TAIL, chunks) - 1) * LANES)
+    end = pl.ds(4 * (chunks - 1) * LANES, 4 * LANES)
 
     def spot(group):
         return pl.ds(pl.multiple_of(flip(own_group, group, groups) * BLOCK, BLOCK), BLOCK)
@@ -242,8 +253,12 @@
             columns = pl.ds(pl.multiple_of(start * BLOCK, BLOCK), size * BLOCK)
             write(vis_ref.at[:, spot(group), columns], spot(group), columns)
             size //= 2
+    for k in range(4):
+        for part in range(2):
+            tail[part * BLOCK:(part + 1) * BLOCK, k * LANES:(k + 1) * LANES] = unpack_field(held[...], k, part)
     for other in range(groups):
-        gram[other] = acc[other] + product(planes[last, :, span], planes[other, :, span])
+        right = tail[...] if other == last else planes[other, :, end]
+        gram[other] = acc[other] + product(planes[last, :, middle], planes[other, :, middle]) + product(tail[...], right)
     for other in range(groups):
         vis_re, vis_im = weigh(gram[other], gcols[last], grows[other])
         row_strip[other, 0] = vis_re
@@ -268,7 +283,7 @@
     scale = 1.0 / (16.0 * words * 4)
     groups = feeds // BLOCK
     chunks = words // LANES
-    pieces = 4 if rows % 32 == 0 else 1
+    cuts = load_cuts(rows)
     dma = pltpu.SemaphoreType.DMA
     vmem = pl.BlockSpec(memory_space=pltpu.VMEM)
     hbm = pl.BlockSpec(memory_space=pltpu.HBM)
@@ -280,18 +295,19 @@
             pltpu.VMEM((groups, 2 * BLOCK, 2 * BLOCK), jnp.float32),
             pltpu.VMEM((groups, BLOCK, 8), jnp.float32),
             pltpu.VMEM((groups, 2, BLOCK), jnp.float32),
+            pltpu.VMEM((BLOCK, LANES), jnp.int32),
         ],
         in_specs=[hbm] * 3,
-        out_specs=[vmem] * 5,
+        out_specs=[vmem] * 6,
         scratch_shapes=[
             pltpu.SMEM((1, slots), jnp.int32),
             pltpu.VMEM((2, slots, BLOCK), jnp.float32),
-            [pltpu.VMEM((slots, rows // pieces, words), jnp.int32)] * pieces,
+            [pltpu.VMEM((slots, b - a, words), jnp.int32) for a, b in zip(cuts, cuts[1:])],
             pltpu.VMEM((slots, rows, words), jnp.int32),
             pltpu.VMEM((slots, 2, BLOCK), jnp.float32),
             pltpu.VMEM((n, rows, words), jnp.int32),
             pltpu.VMEM((n, 2, BLOCK), jnp.float32),
-            dma, dma, dma((pieces,)), dma, dma((n - 2 * per_group,)), dma((per_group, 2)),
+            dma, dma, dma((len(cuts) - 1,)), dma, dma((n - 2 * per_group,)), dma((per_group, 2)),
             dma((per_group, chunks)), dma, dma,
         ],
         compiler_params=pltpu.CompilerParams(
@@ -300,9 +316,10 @@
     vis = pl.pallas_call(
         write_kernel,
         out_shape=jax.ShapeDtypeStruct((2, feeds, feeds), jnp.float32),
-        in_specs=[vmem] * 5,
+        in_specs=[vmem] * 6,
         out_specs=hbm,
         scratch_shapes=[
+            pltpu.VMEM((2 * BLOCK, 4 * LANES), PLANE),
             pltpu.VMEM((groups, 2 * BLOCK, 2 * BLOCK), jnp.float32),
             pltpu.VMEM((groups, 2, BLOCK, BLOCK), jnp.float32),
             pltpu.VMEM((groups, 2, BLOCK, BLOCK), jnp.float32),

time: 31.3 us -> 31.1 us (level)
  no operation moved by 1% of the time
where the time goes in v5:
time: 31.1 us; the launch traced here: 30.9 us
  Pallas kernels  30.9 us (99%)
    pallas_call x1, Pallas kernels, body(): pl.pallas_call(functools.partial(gather_kernel, n, scale), out_shape=[plt...  27.6 us
    pallas_call x1, Pallas kernels, body(): pl.pallas_call(write_kernel, out_shape=jax.ShapeDtypeStruct((2, feeds, fe...  3.29 us

profile of v5, /device:TPU:0, one launch (start us, length us, event | category | flops | bytes accessed | tf_op | source)
XLA Modules:
  0.0 30.9 jit_solution(13290532246080426805)
XLA Ops:
  0.0 27.6 %shard_map.37 = (f32[2,1024,1024]{2,1,0:T(8,128)S(1)}, bf16[8,256,2048]{2,1,0:T(8,128)(2,1)S(1)}, f32[8,256,256]{2,1,0:T(8,128)S(1)}, f32[8,128,8]{2,1,0:T(8,128...) custom-call(s32[1,8]{1,0:T(1,128)} %map_hbm.1, s32[1,8,128,512]{3,2,1,0:T(8,128)} %volt_hbm.1, f32[2,8,128]{2,1,0:T(8,128)} %bitcast.4), custom_call_target="tpu_custom_call" | custom-call | tf_op jit(solution)/shard_map/pallas_call | solution.py:290
  27.6 3.3 %shard_map.38 = f32[2,1024,1024]{2,1,0:T(8,128)} custom-call(f32[2,1024,1024]{2,1,0:T(8,128)S(1)} %get-tuple-element.11.vis_ref, bf16[8,256,2048]{2,1,0:T(8,128)(2,1)S(1)} %get-tuple-element.12.planes, f32[8,256,256]{2,1,0:T(8,128)S(1)} %get-tuple-element.13.acc, f32[8,128,8]{2,1,0:T(8,128)S(1)} %get-tuple-element.14.gcols, ...), custom_call_target="tpu_custom_call" | custom-call | tf_op jit(solution)/shard_map/pallas_call | solution.py:316

commit v6 on v5

--- a/solution.py
+++ b/solution.py
@@ -127,6 +127,7 @@
     for mask in rest:
         for p, strip in enumerate(strips):
             stage[mask, strip] = volts[p][map_ref[0, flip(me, mask, n)]]
+    for mask in rest:
         if mask // per_group in whole:
             send(stage.at[mask], recv.at[spot(mask)], send_sem, landing(mask // per_group, spot(mask), 0), mask)
     for group in chunked:
@@ -153,8 +154,11 @@
 
         def piece(i, carry):
             start = pl.multiple_of(i * step, step)
-            if rows >= step:
+            if rows == BLOCK:
                 packed = recv[group, pl.ds(start, step), part_of]
+            elif rows >= step:
+                inner = pl.multiple_of(lax.rem(start, rows), step)
+                packed = recv[group * per_group + start // rows, pl.ds(inner, step), part_of]
             else:
                 first = group * per_group + i * (step // rows)
                 packed = recv[pl.ds(first, step // rows), :, part_of].reshape(step, LANES)

time: 31.1 us -> 31.1 us (level)
  no operation moved by 1% of the time
where the time goes in v6:
time: 31.1 us; the launch traced here: 30.9 us
  Pallas kernels  30.9 us (99%)
    pallas_call x1, Pallas kernels, body(): pl.pallas_call(functools.partial(gather_kernel, n, scale), out_shape=[plt...  27.6 us
    pallas_call x1, Pallas kernels, body(): pl.pallas_call(write_kernel, out_shape=jax.ShapeDtypeStruct((2, feeds, fe...  3.29 us

profile of v6, /device:TPU:0, one launch (start us, length us, event | category | flops | bytes accessed | tf_op | source)
XLA Modules:
  0.0 30.9 jit_solution(369223950254554510)
XLA Ops:
  0.0 27.6 %shard_map.37 = (f32[2,1024,1024]{2,1,0:T(8,128)S(1)}, bf16[8,256,2048]{2,1,0:T(8,128)(2,1)S(1)}, f32[8,256,256]{2,1,0:T(8,128)S(1)}, f32[8,128,8]{2,1,0:T(8,128...) custom-call(s32[1,8]{1,0:T(1,128)} %map_hbm.1, s32[1,8,128,512]{3,2,1,0:T(8,128)} %volt_hbm.1, f32[2,8,128]{2,1,0:T(8,128)} %bitcast.4), custom_call_target="tpu_custom_call" | custom-call | tf_op jit(solution)/shard_map/pallas_call | solution.py:294
  27.6 3.3 %shard_map.38 = f32[2,1024,1024]{2,1,0:T(8,128)} custom-call(f32[2,1024,1024]{2,1,0:T(8,128)S(1)} %get-tuple-element.11.vis_ref, bf16[8,256,2048]{2,1,0:T(8,128)(2,1)S(1)} %get-tuple-element.12.planes, f32[8,256,256]{2,1,0:T(8,128)S(1)} %get-tuple-element.13.acc, f32[8,128,8]{2,1,0:T(8,128)S(1)} %get-tuple-element.14.gcols, ...), custom_call_target="tpu_custom_call" | custom-call | tf_op jit(solution)/shard_map/pallas_call | solution.py:320

commit v7 on v6

--- a/solution.py
+++ b/solution.py
@@ -15,7 +15,7 @@
 
 
 def load_cuts(rows):
-    return [0, rows // 8, rows // 2, rows] if rows % 64 == 0 else [0, rows]
+    return [0, rows // 8, rows] if rows % 64 == 0 else [0, rows]
 
 
 def unpack_field(packed, k, part):
@@ -90,6 +90,7 @@
     order = send_order(n)
     lead, rest = order[:2], order[2:]
     pair = max(chunks // 2, 1)
+    own = 1 if per_group == 1 else 0
 
     def send(source, target, sent, landed, mask):
         pltpu.make_async_remote_copy(
@@ -102,7 +103,7 @@
             return last_sem.at[inner, c]
         if group in chunked:
             return half_sem.at[inner, c // pair]
-        return whole_sem.at[whole.index(group) * per_group + inner]
+        return whole_sem.at[whole.index(group) * per_group + inner - own]
 
     def spot(mask):
         return (mask // per_group) * per_group + low
@@ -131,8 +132,9 @@
         if mask // per_group in whole:
             send(stage.at[mask], recv.at[spot(mask)], send_sem, landing(mask // per_group, spot(mask), 0), mask)
     for group in chunked:
-        for c in range(chunks):
-            part = pl.ds(c * LANES, LANES)
+        width = 1 if group == last else pair
+        for c in range(0, chunks, width):
+            part = pl.ds(c * LANES, width * LANES)
             for mask in rest:
                 if mask // per_group == group:
                     send(stage.at[mask, :, part], recv.at[spot(mask), :, part], send_sem,
@@ -311,7 +313,7 @@
             pltpu.VMEM((slots, 2, BLOCK), jnp.float32),
             pltpu.VMEM((n, rows, words), jnp.int32),
             pltpu.VMEM((n, 2, BLOCK), jnp.float32),
-            dma, dma, dma((len(cuts) - 1,)), dma, dma((n - 2 * per_group,)), dma((per_group, 2)),
+            dma, dma, dma((len(cuts) - 1,)), dma, dma((n - 2 * per_group - (per_group == 1),)), dma((per_group, 2)),
             dma((per_group, chunks)), dma, dma,
         ],
         compiler_params=pltpu.CompilerParams(

time: 31.1 us -> 31.4 us (level)
  Pallas kernels: 30.9 us -> 31.3 us
    pallas_call x1, Pallas kernels: 27.6 us -> 28 us  [body(): pl.pallas_call(functools.partial(gather_kernel, n, scale), out_shape=[plt...]
where the time goes in v7:
time: 31.4 us; the launch traced here: 31.3 us
  Pallas kernels  31.3 us (100%)
    pallas_call x1, Pallas kernels, body(): pl.pallas_call(functools.partial(gather_kernel, n, scale), out_shape=[plt...  28 us
    pallas_call x1, Pallas kernels, body(): pl.pallas_call(write_kernel, out_shape=jax.ShapeDtypeStruct((2, feeds, fe...  3.29 us

profile of v7, /device:TPU:0, one launch (start us, length us, event | category | flops | bytes accessed | tf_op | source)
XLA Modules:
  0.0 31.3 jit_solution(12417365276564208235)
XLA Ops:
  0.0 28.0 %shard_map.37 = (f32[2,1024,1024]{2,1,0:T(8,128)S(1)}, bf16[8,256,2048]{2,1,0:T(8,128)(2,1)S(1)}, f32[8,256,256]{2,1,0:T(8,128)S(1)}, f32[8,128,8]{2,1,0:T(8,128...) custom-call(s32[1,8]{1,0:T(1,128)} %map_hbm.1, s32[1,8,128,512]{3,2,1,0:T(8,128)} %volt_hbm.1, f32[2,8,128]{2,1,0:T(8,128)} %bitcast.4), custom_call_target="tpu_custom_call" | custom-call | tf_op jit(solution)/shard_map/pallas_call | solution.py:296
  28.0 3.3 %shard_map.38 = f32[2,1024,1024]{2,1,0:T(8,128)} custom-call(f32[2,1024,1024]{2,1,0:T(8,128)S(1)} %get-tuple-element.11.vis_ref, bf16[8,256,2048]{2,1,0:T(8,128)(2,1)S(1)} %get-tuple-element.12.planes, f32[8,256,256]{2,1,0:T(8,128)S(1)} %get-tuple-element.13.acc, f32[8,128,8]{2,1,0:T(8,128)S(1)} %get-tuple-element.14.gcols, ...), custom_call_target="tpu_custom_call" | custom-call | tf_op jit(solution)/shard_map/pallas_call | solution.py:322
